TPU v7x, 128 devices: a whole 4x4x4 slice. The times are simulated.
128 devices in a mesh: dp: 16 (over x, y), mp: 8 (over z, core).
Axes of the slice: x: 4, y: 4, z: 4, core: 2. Of those that a mesh axis runs over, the one named last changes fastest.
Arguments:
- activations: bfloat16 [16384, 4096], P(('dp', 'mp')), may hold values from -17 to 17
- output_grads: bfloat16 [16384, 14336], P('dp', 'mp'), may hold values from -0.046875 to 0.046875
- q_start: float32 [14336, 64], P('mp'), may hold values from -6 to 6
Outputs:
- new_error: bfloat16 [65536, 14336], P('dp', 'mp')
- q_factor: float32 [14336, 64], P('mp')
All inputs are finite; a program needn't handle non-finite values.
Results may differ from a plain program's by a relative error of at most 0.01.
Values may be sent and summed in bfloat16 or wider, within the bound.
A program may use at most 192 MiB of HBM per device.

v0:
```python
import jax
import jax.numpy as jnp
from jax import lax
from jax.sharding import PartitionSpec as P


def split_up(value, dim, count):
    before, after = (value.shape[:dim], value.shape[dim + 1 :])
    return jnp.moveaxis(value.reshape(*before, count, -1, *after), dim, 0)


def summed_on_arrival(value, axis, dim):
    count = lax.axis_size(axis)
    blocks = lax.all_to_all(split_up(value, dim, count), axis, 0, 0, tiled=True)
    return jnp.sum(blocks, axis=0)


def copy_for_each(value, axis):
    count = lax.axis_size(axis)
    return lax.all_to_all(
        jnp.broadcast_to(value[None], (count, *value.shape)), axis, 0, 0, tiled=True
    )


def taken_together(value, axis):
    return copy_for_each(value, axis).sum(axis=0)


def laid_out(blocks, dim):
    blocks = jnp.moveaxis(blocks, 0, dim)
    shape = blocks.shape
    return blocks.reshape(*shape[:dim], shape[dim] * shape[dim + 1], *shape[dim + 2 :])


def collect(value, axis, dim):
    return laid_out(copy_for_each(value, axis), dim)


def orthonormal(p_mean, gram_matrix):
    lower_tri = jnp.linalg.cholesky(gram_matrix)
    return lax.linalg.triangular_solve(
        lower_tri, p_mean, left_side=False, lower=True, transpose_a=True
    )


def split_parts(values):
    upper = values.astype(jnp.bfloat16)
    lower = (values - upper.astype(jnp.float32)).astype(jnp.bfloat16)
    return (upper, lower)


def per_device(activations, output_grads, q_start):
    contract_rows = (((0,), (0,)), ((), ()))
    replicas = lax.axis_size("dp")
    gathered = lax.all_gather(activations, "mp", axis=0, tiled=True)
    q_upper, q_lower = split_parts(q_start)
    projected = jnp.dot(output_grads, q_upper, preferred_element_type=jnp.float32)
    projected = projected + jnp.dot(output_grads, q_lower, preferred_element_type=jnp.float32)
    proj_upper, proj_lower = split_parts(projected)
    partial_p = lax.dot_general(
        gathered, proj_upper, contract_rows, preferred_element_type=jnp.float32
    )
    partial_p = partial_p + lax.dot_general(
        gathered, proj_lower, contract_rows, preferred_element_type=jnp.float32
    )
    gradient = lax.dot_general(
        gathered, output_grads, contract_rows, preferred_element_type=jnp.float32
    )
    row_block = summed_on_arrival(partial_p, "mp", 0)
    row_block = taken_together(row_block, "dp") / replicas
    block_gram = lax.dot_general(row_block, row_block, contract_rows)
    gram_matrix = taken_together(block_gram, "mp")
    ortho_rows = orthonormal(row_block, gram_matrix)
    p_ortho = collect(ortho_rows, "mp", 0)
    local_factor = lax.dot_general(gradient, p_ortho, contract_rows)
    q_factor = lax.psum(local_factor, "dp") / replicas
    decompressed = lax.dot_general(p_ortho, q_factor, (((1,), (1,)), ((), ())))
    new_error = (gradient - decompressed).astype(jnp.bfloat16)
    return (new_error, q_factor)


def solution(mesh):
    in_specs = (P(("dp", "mp"), None), P("dp", "mp"), P("mp", None))
    out_specs = (P("dp", "mp"), P("mp", None))
    return jax.shard_map(
        per_device, mesh=mesh, in_specs=in_specs, out_specs=out_specs, check_vma=False
    )
```

profile of v0, /device:TPU:0, one launch (start us, length us, event | category | flops | bytes accessed | tf_op | source)
XLA Modules:
  0.0 294.8 jit_solution(3268212242968762611)
XLA Ops:
  7.2 0.7 all-gather.2.cloned.1.call-update
  7.9 3.6 %convolution_bitcast_fusion = f32[1024,64]{0,1:T(8,128)S(1)} fusion(bf16[1024,1792]{1,0:T(8,128)(2,1)} %param.4, f32[1792,64]{0,1:T(8,128)} %param.5), kind=kOutput, calls=%fused_computation.3 | convolution fusion | flops 235339776 | bytes 4390912 | tf_op jit(solution)/shard_map/dot_general | solution.py:58
  11.5 3.4 %convolution_add_fusion.1 = f32[1024,64]{0,1:T(8,128)S(1)} fusion(f32[1024,64]{0,1:T(8,128)S(1)} %convolution_bitcast_fusion, bf16[1024,1792]{1,0:T(8,128)(2,1)} %param.4, f32[1792,64]{0,1:T(8,128)} %param.5), kind=kOutput, calls=%fused_computation.2 | convolution fusion | flops 235061248 | bytes 4653056 | tf_op jit(solution)/shard_map/dot_general | solution.py:57
  14.8 47.3 %all-gather.2.cloned.1.call-done = bf16[1024,4096]{1,0:T(8,128)(2,1)} async-done(((bf16[128,4096]{1,0:T(8,128)(2,1)}), bf16[1024,4096]{1,0:T(8,128)(2,1)}) %all-gather.2.cloned.1.call-update) | async-done | bytes 8388624 | tf_op jit(solution)/shard_map/all_gather | solution.py:55
  62.1 5.1 %fusion.9 = f32[64,4096]{1,0:T(8,128)S(1)} fusion(bf16[1024,4096]{1,0:T(8,128)(2,1)} %all-gather.2.cloned.1.call-done, f32[1024,64]{0,1:T(8,128)S(1)} %convolution_add_fusion.1), kind=kOutput, calls=%fused_computation.17 | convolution fusion | flops 536936448 | bytes 9699328 | tf_op jit(solution)/shard_map/dot_general | solution.py:60
  67.2 0.7 copy-done
  67.9 1.6 convolution_add_fusion
  69.4 0.1 copy.26
  69.5 19.0 %all_to_all.20 = f32[8,512,64]{1,2,0:T(8,128)S(1)} all-to-all(f32[8,512,64]{1,2,0:T(8,128)S(1)} %bitcast.31), channel_id=1, replica_groups=mesh['dp'=16,'mp'=8] {'mp'}, dimensions={0} | all-to-all | bytes 2097152 | tf_op jit(solution)/shard_map/all_to_all | solution.py:14
  88.5 0.1 reduce_sum.27
  88.6 0.3 broadcast_in_dim.7
  88.8 34.6 %all_to_all.21 = f32[16,512,64]{1,2,0:T(8,128)S(1)} all-to-all(f32[16,512,64]{1,2,0:T(8,128)S(1)} %broadcast_in_dim.7), channel_id=1, replica_groups=mesh['dp'=16,'mp'=8] {'dp'}, dimensions={0} | all-to-all | bytes 4194304 | tf_op jit(solution)/shard_map/all_to_all | solution.py:20
  123.4 0.2 reduce_sum.28
  123.6 0.1 fusion.2
  123.8 0.2 reshape.24
  123.9 8.5 %all_to_all.22 = f32[8,1,4096]{2,1,0:T(1,128)S(1)} all-to-all(f32[8,1,4096]{2,1,0:T(1,128)S(1)} %reshape.24), channel_id=1, replica_groups=mesh['dp'=16,'mp'=8] {'mp'}, dimensions={0} | all-to-all | bytes 262144 | tf_op jit(solution)/shard_map/all_to_all | solution.py:20
  132.4 0.5 broadcast.52
  132.9 1.0 reduce.6
  133.9 0.1 reshape.25
  134.1 5.8 %cholesky.16 = f32[64,64]{1,0:T(8,128)S(1)} custom-call(f32[64,64]{1,0:T(8,128)S(1)} %fusion.13), custom_call_target="Cholesky" | custom-call | tf_op jit(solution)/shard_map/jit(cholesky)/cholesky | solution.py:40
  140.0 0.6 compare_reduce_fusion
  140.7 0.7 fusion.11
  141.3 4.9 %custom-call.6 = f32[1,64,64]{1,2,0:T(8,128)S(1)} custom-call(f32[1,64,64]{2,1,0:T(8,128)S(1)} %fusion.11), custom_call_target="InvertDiagBlocksLowerTriangular" | custom-call | tf_op jit(solution)/shard_map/triangular_solve | solution.py:41
  146.2 0.3 fusion
  146.5 0.8 broadcast_in_dim.10
  147.4 3.5 %all-to-all-start.3 = ((bf16[8,512,64]{1,2,0:T(8,128)(2,1)}), bf16[8,512,64]{1,2,0:T(8,128)(2,1)S(1)}, u32[]{:S(2)}, u32[]{:S(2)}) async-start(bf16[8,512,64]{1,2,0:T(8,128)(2,1)} %broadcast_in_dim.10), calls=%async_computation.3 | async-start | bytes 1048576 | tf_op jit(solution)/shard_map/all_to_all | solution.py:20
  150.9 0.2 all-reduce.2.cloned.1.call-start
  151.1 22.9 %fusion.16 = f32[4096,1792]{1,0:T(8,128)} fusion(bf16[1024,4096]{1,0:T(8,128)(2,1)} %all-gather.2.cloned.1.call-done, bf16[1024,1792]{1,0:T(8,128)(2,1)} %param.4), kind=kOutput, calls=%fused_computation.30 | convolution fusion | flops 15032385536 | bytes 41418752 | tf_op jit(solution)/shard_map/dot_general | solution.py:66
  174.0 12.8 %fusion.17 = f32[1792,64]{0,1:T(8,128)} fusion(f32[4096,1792]{1,0:T(8,128)} %fusion.16, bf16[4096,64]{0,1:T(8,128)(2,1)S(1)} %bitcast.28), kind=kOutput, calls=%fused_computation.31 | convolution fusion | flops 939524096 | bytes 30343168 | tf_op jit(solution)/shard_map/dot_general | solution.py:75
  186.8 82.8 %all-reduce.2.cloned.1.call-done = f32[1792,64]{0,1:T(8,128)} async-done(((f32[1792,64]{0,1:T(8,128)}), f32[1792,64]{0,1:T(8,128)}) %all-reduce.2.cloned.1.call-update) | async-done | bytes 458768 | tf_op jit(solution)/shard_map/psum | solution.py:76
  269.6 1.0 broadcast_multiply_fusion
  270.7 17.3 %subtract_convert_fusion = bf16[4096,1792]{1,0:T(8,128)(2,1)} fusion(f32[4096,1792]{1,0:T(8,128)} %fusion.16, bf16[4096,64]{0,1:T(8,128)(2,1)S(1)} %bitcast.29, f32[1792,64]{0,1:T(8,128)S(1)} %broadcast_multiply_fusion), kind=kOutput, calls=%fused_computation | convolution fusion | flops 954204160 | bytes 45023232 | tf_op jit(solution)/shard_map/dot_general | solution.py:77
  (12 shorter events, 0.3 us)
Async XLA Ops:
  7.2 54.9 %all-gather.2.cloned.1.call-start = ((), (), s32[]{:S(2)}) async-start(), calls=%async_computation.4 | async-start | bytes 9437184 | tf_op jit(solution)/shard_map/all_gather | solution.py:55
  62.1 5.8 %copy-start = (bf16[1024,4096]{1,0:T(8,128)(2,1)S(1)}, bf16[1024,4096]{1,0:T(8,128)(2,1)}, u32[]{:S(2)}) copy-start(bf16[1024,4096]{1,0:T(8,128)(2,1)} %all-gather.2.cloned.1.call-done) | copy-start | bytes 25165828
  147.4 26.6 %all-to-all-start.3 = ((bf16[8,512,64]{1,2,0:T(8,128)(2,1)}), bf16[8,512,64]{1,2,0:T(8,128)(2,1)S(1)}, u32[]{:S(2)}, u32[]{:S(2)}) async-start(bf16[8,512,64]{1,2,0:T(8,128)(2,1)} %broadcast_in_dim.10), calls=%async_computation.3 | async-start | bytes 1048576 | tf_op jit(solution)/shard_map/all_to_all | solution.py:20
  150.9 118.7 %all-reduce.2.cloned.1.call-start = ((), (), s32[]{:S(2)}) async-start(), calls=%async_computation.5 | async-start | bytes 917504 | tf_op jit(solution)/shard_map/psum | solution.py:76
  270.7 17.3 %copy-start.1 = (f32[1792,64]{0,1:T(8,128)}, f32[1792,64]{0,1:T(8,128)S(1)}, u32[]{:S(2)}) copy-start(f32[1792,64]{0,1:T(8,128)S(1)} %broadcast_multiply_fusion) | copy-start | bytes 1376260
Sparse Core Ops, SparseCore 0:
  9.7 52.3 all-gather.1
  186.9 82.6 all-reduce.1
where the time goes:
time: 295 us
  waiting for transfers between devices  131 us (44%)
  matrix products  67 us (23%)
  blocking collectives  62 us (21%)
  other arithmetic  14.3 us (5%)
  between operations  14.2 us (5%)
  starting transfers between devices  3.75 us (1%)
    psum x1, waiting for transfers between devices, per_device(): q_factor = lax.psum(local_factor, 'dp') / replicas  82.8 us
    all_gather x1, waiting for transfers between devices, per_device(): gathered = lax.all_gather(activations, 'mp', axis=0, tiled=True)  47.3 us
    all_to_all x2, blocking collectives, copy_for_each(): lax.all_to_all(jnp.broadcast_to(value[None], (count, *value.shape)), axis...  43.1 us
    dot_general x1, matrix products, per_device(): lax.dot_general(gathered, output_grads, contract_rows, preferred_element_...  22.9 us
    all_to_all x1, blocking collectives, summed_on_arrival(): blocks = lax.all_to_all(split_up(value, dim, count), axis, 0, 0, tiled=True)  19 us
    dot_general x1, matrix products, per_device(): decompressed = lax.dot_general(p_ortho, q_factor, (((1,), (1,)), ((), ())))  17.3 us
    dot_general x1, matrix products, per_device(): local_factor = lax.dot_general(gradient, p_ortho, contract_rows)  12.8 us
    another operation x3, other arithmetic, orthonormal(): lower_tri = jnp.linalg.cholesky(gram_matrix)  6.52 us
  transfers between devices with their start and end apart: 3, of which 2 were waited for; matrix products, arithmetic and copies ran while one was open for 10% of the time, Pallas kernels for 0%

commit v1 on v0

--- a/solution.py
+++ b/solution.py
@@ -52,7 +52,31 @@
 def per_device(activations, output_grads, q_start):
     contract_rows = (((0,), (0,)), ((), ()))
     replicas = lax.axis_size("dp")
-    gathered = lax.all_gather(activations, "mp", axis=0, tiled=True)
+    extra, v_now, z2 = (lax.psum(1, axis_name="mp"), lax.axis_index("mp"), activations.shape[0])
+    local_out = clean = activations
+    gathered = lax.dynamic_update_slice_in_dim(
+        jnp.zeros(
+            tuple((i0 * extra if rr == 0 else i0 for rr, i0 in enumerate(activations.shape))),
+            activations.dtype,
+        ),
+        activations,
+        v_now * z2,
+        axis=0,
+    )
+    for ii in range(1, extra // 2 + 1):
+        local_out = lax.ppermute(
+            local_out, axis_name="mp", perm=tuple(((rr, (rr + 1) % extra) for rr in range(extra)))
+        )
+        gathered = lax.dynamic_update_slice_in_dim(
+            gathered, local_out, (v_now - ii) % extra * z2, axis=0
+        )
+        if 2 * ii < extra:
+            clean = lax.ppermute(
+                clean, axis_name="mp", perm=tuple(((rr, (rr - 1) % extra) for rr in range(extra)))
+            )
+            gathered = lax.dynamic_update_slice_in_dim(
+                gathered, clean, (v_now + ii) % extra * z2, axis=0
+            )
     q_upper, q_lower = split_parts(q_start)
     projected = jnp.dot(output_grads, q_upper, preferred_element_type=jnp.float32)
     projected = projected + jnp.dot(output_grads, q_lower, preferred_element_type=jnp.float32)

time: 295 us -> 307 us (1.041)
  local copies, waits for them, and re-layouts: 2.78 us -> 17.4 us
  waiting for transfers between devices: 131 us -> 117 us
  starting transfers between devices: 3.75 us -> 13.4 us
    all_gather x1 -> x0, waiting for transfers between devices: 47.3 us -> none  [per_device(): gathered = lax.all_gather(activations, 'mp', axis=0, tiled=True)]
    ppermute x0 -> x7, waiting for transfers between devices: none -> 34.4 us  [the longest x4 22.9 us: per_device(): lax.ppermute(local_out, axis_name='mp', perm=tuple(((rr, (rr + 1) % extra...]
    dynamic_update_slice x0 -> x8, local copies, waits for them, and re-layouts: none -> 10.8 us  [the longest x4 6.65 us: per_device(): lax.dynamic_update_slice_in_dim(gathered, local_out, (v_now - ii) % extra...]
    ppermute x0 -> x7, starting transfers between devices: none -> 9.7 us  [the longest x3 9.67 us: per_device(): lax.ppermute(clean, axis_name='mp', perm=tuple(((rr, (rr - 1) % extra) fo...]
    broadcast_in_dim x0 -> x1, local copies, waits for them, and re-layouts: none -> 4.45 us  [per_device(): jnp.zeros(tuple((i0 * extra if rr == 0 else i0 for rr, i0 in enumerate(ac...]
    dot_general x1, matrix products: 1.57 us -> 4.94 us  [per_device(): lax.dot_general(gathered, proj_lower, contract_rows, preferred_element_ty...]
  transfers between devices with their start and end apart: 3 -> 9, of which waited for: 2 -> 7; matrix products, arithmetic and copies ran while one was open for 10% -> 14% of each run, Pallas kernels for 0% -> 0%
where the time goes in v1:
time: 307 us; the launch traced here: 306 us
  waiting for transfers between devices  117 us (38%)
  matrix products  68.1 us (22%)
  blocking collectives  61.7 us (20%)
  local copies, waits for them, and re-layouts  17.4 us (6%)
  other arithmetic  14.3 us (5%)
  between operations  14.3 us (5%)
  starting transfers between devices  13.4 us (4%)
    psum x1, waiting for transfers between devices, per_device(): q_factor = lax.psum(local_factor, 'dp') / replicas  82.7 us
    all_to_all x2, blocking collectives, copy_for_each(): lax.all_to_all(jnp.broadcast_to(value[None], (count, *value.shape)), axis...  43.3 us
    ppermute x4, waiting for transfers between devices, per_device(): lax.ppermute(local_out, axis_name='mp', perm=tuple(((rr, (rr + 1) % extra...  22.9 us
    dot_general x1, matrix products, per_device(): lax.dot_general(gathered, output_grads, contract_rows, preferred_element_...  22.9 us
    all_to_all x1, blocking collectives, summed_on_arrival(): blocks = lax.all_to_all(split_up(value, dim, count), axis, 0, 0, tiled=True)  18.4 us
    dot_general x1, matrix products, per_device(): decompressed = lax.dot_general(p_ortho, q_factor, (((1,), (1,)), ((), ())))  17.3 us
    dot_general x1, matrix products, per_device(): local_factor = lax.dot_general(gradient, p_ortho, contract_rows)  12.8 us
    ppermute x3, waiting for transfers between devices, per_device(): lax.ppermute(clean, axis_name='mp', perm=tuple(((rr, (rr - 1) % extra) fo...  11.5 us
  transfers between devices with their start and end apart: 9, of which 7 were waited for; matrix products, arithmetic and copies ran while one was open for 14% of the time, Pallas kernels for 0%

profile of v1, /device:TPU:0, one launch (start us, length us, event | category | flops | bytes accessed | tf_op | source)
XLA Modules:
  0.0 306.5 jit_solution(5101942436973597551)
XLA Ops:
  7.2 3.6 %collective-permute-start.1 = (bf16[128,4096]{1,0:T(8,128)(2,1)}, bf16[128,4096]{1,0:T(8,128)(2,1)S(1)}, u32[]{:S(2)}, u32[]{:S(2)}) collective-permute-start(bf16[128,4096]{1,0:T(8,128)(2,1)} %param.3), channel_id=1, source_target_pairs={{0,7},{1,0},{2,1},{3,2},{4,3},{5,4},{6,5},{7,6},{8,15},{9,8},{10,9... | collective-permute-start | bytes 3145736 | tf_op jit(solution)/shard_map/ppermute | solution.py:74
  10.8 12.8 %collective-permute-done = bf16[128,4096]{1,0:T(8,128)(2,1)} collective-permute-done((bf16[128,4096]{1,0:T(8,128)(2,1)}, bf16[128,4096]{1,0:T(8,128)(2,1)}, u32[]{:S(2)}, u32[]{:S(2)}) %collective-permute-start) | collective-permute-done | bytes 1048608 | tf_op jit(solution)/shard_map/ppermute | solution.py:67
  23.6 3.6 %convolution_bitcast_fusion = f32[1024,64]{0,1:T(8,128)S(1)} fusion(bf16[1024,1792]{1,0:T(8,128)(2,1)} %param.4, f32[1792,64]{0,1:T(8,128)} %param.5), kind=kOutput, calls=%fused_computation.3 | convolution fusion | flops 235339776 | bytes 4390912 | tf_op jit(solution)/shard_map/dot_general | solution.py:82
  27.2 4.4 %broadcast_in_dim.9 = bf16[1024,4096]{1,0:T(8,128)(2,1)} broadcast(bf16[]{:T(256)} %constant.91.clone.1), dimensions={} | broadcast | bytes 8388610 | tf_op jit(solution)/shard_map/broadcast_in_dim | solution.py:58
  31.6 1.0 constant_dynamic-update-slice_fusion.7
  32.7 3.0 collective-permute-start.3
  35.6 1.2 convolution_add_fusion.1
  37.0 2.4 collective-permute-done.2
  39.4 2.3 constant_dynamic-update-slice_fusion.6
  41.7 1.0 constant_dynamic-update-slice_fusion.5
  42.7 5.2 %collective-permute-done.3 = bf16[128,4096]{1,0:T(8,128)(2,1)S(1)} collective-permute-done((bf16[128,4096]{1,0:T(8,128)(2,1)S(1)}, bf16[128,4096]{1,0:T(8,128)(2,1)S(1)}, u32[]{:S(2)}, u32[]{:S(2)}) %collective-permute-start.3) | collective-permute-done | bytes 1048608 | tf_op jit(solution)/shard_map/ppermute | solution.py:74
  48.0 3.1 %collective-permute-start.5 = (bf16[128,4096]{1,0:T(8,128)(2,1)S(1)}, bf16[128,4096]{1,0:T(8,128)(2,1)S(1)}, u32[]{:S(2)}, u32[]{:S(2)}) collective-permute-start(bf16[128,4096]{1,0:T(8,128)(2,1)S(1)} %collective-permute-done.3), channel_id=1, source_target_pairs={{0,7},{1,0},{2,1},{3,2},{4,3},{5,4},{6,5},{7,6},{8,15},{9,8},{10,9... | collective-permute-start | bytes 3145736 | tf_op jit(solution)/shard_map/ppermute | solution.py:74
  51.1 2.3 constant_dynamic-update-slice_fusion.4
  53.4 1.7 collective-permute-done.4
  55.0 1.0 constant_dynamic-update-slice_fusion.3
  56.1 1.0 constant_dynamic-update-slice_fusion.2
  57.1 6.3 %collective-permute-done.5 = bf16[128,4096]{1,0:T(8,128)(2,1)S(1)} collective-permute-done((bf16[128,4096]{1,0:T(8,128)(2,1)S(1)}, bf16[128,4096]{1,0:T(8,128)(2,1)S(1)}, u32[]{:S(2)}, u32[]{:S(2)}) %collective-permute-start.5) | collective-permute-done | bytes 1048608 | tf_op jit(solution)/shard_map/ppermute | solution.py:74
  64.4 6.0 %collective-permute-done.6 = bf16[128,4096]{1,0:T(8,128)(2,1)S(1)} collective-permute-done((bf16[128,4096]{1,0:T(8,128)(2,1)S(1)}, bf16[128,4096]{1,0:T(8,128)(2,1)S(1)}, u32[]{:S(2)}, u32[]{:S(2)}) %collective-permute-start.6) | collective-permute-done | bytes 1048608 | tf_op jit(solution)/shard_map/ppermute | solution.py:67
  70.5 1.0 constant_dynamic-update-slice_fusion
  71.5 4.9 %fusion = f32[4096,64]{0,1:T(8,128)S(1)} fusion(bf16[1024,4096]{1,0:T(8,128)(2,1)} %constant_dynamic-update-slice_fusion, f32[1024,64]{0,1:T(8,128)S(1)} %convolution_add_fusion.1), kind=kOutput, calls=%fused_computation.8 | convolution fusion | flops 537133056 | bytes 9699328 | tf_op jit(solution)/shard_map/dot_general | solution.py:87
  76.4 5.0 %convolution_add_fusion = f32[4096,64]{0,1:T(8,128)S(1)} fusion(f32[4096,64]{0,1:T(8,128)S(1)} %fusion, bf16[1024,4096]{1,0:T(8,128)(2,1)} %constant_dynamic-update-slice_fusion, f32[1024,64]{0,1:T(8,128)S(1)} %convolution_add_fusion.1), kind=kOutput, calls=%fused_computation.1 | convolution fusion | flops 537198592 | bytes 10747904 | tf_op jit(solution)/shard_map/dot_general | solution.py:84
  81.5 18.4 %all_to_all.20 = f32[8,512,64]{1,2,0:T(8,128)S(1)} all-to-all(f32[8,512,64]{1,2,0:T(8,128)S(1)} %bitcast.30), channel_id=1, replica_groups=mesh['dp'=16,'mp'=8] {'mp'}, dimensions={0} | all-to-all | bytes 2097152 | tf_op jit(solution)/shard_map/all_to_all | solution.py:14
  100.3 34.8 %all_to_all.21 = f32[16,512,64]{1,2,0:T(8,128)S(1)} all-to-all(f32[16,512,64]{1,2,0:T(8,128)S(1)} %broadcast_in_dim.11), channel_id=1, replica_groups=mesh['dp'=16,'mp'=8] {'dp'}, dimensions={0} | all-to-all | bytes 4194304 | tf_op jit(solution)/shard_map/all_to_all | solution.py:20
  135.6 8.5 %all_to_all.22 = f32[8,1,4096]{2,1,0:T(1,128)S(1)} all-to-all(f32[8,1,4096]{2,1,0:T(1,128)S(1)} %reshape.24), channel_id=1, replica_groups=mesh['dp'=16,'mp'=8] {'mp'}, dimensions={0} | all-to-all | bytes 262144 | tf_op jit(solution)/shard_map/all_to_all | solution.py:20
  145.8 5.8 %cholesky.16 = f32[64,64]{1,0:T(8,128)S(1)} custom-call(f32[64,64]{1,0:T(8,128)S(1)} %fusion.13), custom_call_target="Cholesky" | custom-call | tf_op jit(solution)/shard_map/jit(cholesky)/cholesky | solution.py:40
  153.0 4.9 %custom-call.6 = f32[1,64,64]{1,2,0:T(8,128)S(1)} custom-call(f32[1,64,64]{2,1,0:T(8,128)S(1)} %fusion.11), custom_call_target="InvertDiagBlocksLowerTriangular" | custom-call | tf_op jit(solution)/shard_map/triangular_solve | solution.py:41
  159.1 3.5 %all-to-all-start.3 = ((bf16[8,512,64]{1,2,0:T(8,128)(2,1)}), bf16[8,512,64]{1,2,0:T(8,128)(2,1)S(1)}, u32[]{:S(2)}, u32[]{:S(2)}) async-start(bf16[8,512,64]{1,2,0:T(8,128)(2,1)} %broadcast_in_dim.13), calls=%async_computation.3 | async-start | bytes 1048576 | tf_op jit(solution)/shard_map/all_to_all | solution.py:20
  162.8 22.9 %fusion.16 = f32[4096,1792]{1,0:T(8,128)} fusion(bf16[1024,4096]{1,0:T(8,128)(2,1)} %constant_dynamic-update-slice_fusion, bf16[1024,1792]{1,0:T(8,128)(2,1)} %param.4), kind=kOutput, calls=%fused_computation.38 | convolution fusion | flops 15032385536 | bytes 41418752 | tf_op jit(solution)/shard_map/dot_general | solution.py:90
  185.7 12.8 %fusion.17 = f32[1792,64]{0,1:T(8,128)} fusion(f32[4096,1792]{1,0:T(8,128)} %fusion.16, bf16[4096,64]{0,1:T(8,128)(2,1)S(1)} %bitcast.27), kind=kOutput, calls=%fused_computation.39 | convolution fusion | flops 939524096 | bytes 30343168 | tf_op jit(solution)/shard_map/dot_general | solution.py:99
  198.5 82.7 %all-reduce.2.cloned.1.call-done = f32[1792,64]{0,1:T(8,128)} async-done(((f32[1792,64]{0,1:T(8,128)}), f32[1792,64]{0,1:T(8,128)}) %all-reduce.2.cloned.1.call-update) | async-done | bytes 458768 | tf_op jit(solution)/shard_map/psum | solution.py:100
  281.3 1.0 broadcast_multiply_fusion
  282.3 17.3 %subtract_convert_fusion = bf16[4096,1792]{1,0:T(8,128)(2,1)} fusion(f32[4096,1792]{1,0:T(8,128)} %fusion.16, bf16[4096,64]{0,1:T(8,128)(2,1)S(1)} %bitcast.28, f32[1792,64]{0,1:T(8,128)S(1)} %broadcast_multiply_fusion), kind=kOutput, calls=%fused_computation | convolution fusion | flops 954204160 | bytes 45023232 | tf_op jit(solution)/shard_map/dot_general | solution.py:101
  (36 shorter events, 6.5 us)
Async XLA Ops:
  7.2 24.5 %copy-start.3 = (bf16[128,4096]{1,0:T(8,128)(2,1)S(1)}, bf16[128,4096]{1,0:T(8,128)(2,1)}, u32[]{:S(2)}) copy-start(bf16[128,4096]{1,0:T(8,128)(2,1)} %param.3) | copy-start | bytes 3145732
  7.2 28.5 %copy-start.1 = (f32[1792,64]{0,1:T(8,128)S(1)}, f32[1792,64]{0,1:T(8,128)}, u32[]{:S(2)}) copy-start(f32[1792,64]{0,1:T(8,128)} %param.5) | copy-start | bytes 1376260
  7.2 16.4 %collective-permute-start = (bf16[128,4096]{1,0:T(8,128)(2,1)}, bf16[128,4096]{1,0:T(8,128)(2,1)}, u32[]{:S(2)}, u32[]{:S(2)}) collective-permute-start(bf16[128,4096]{1,0:T(8,128)(2,1)} %param.3), channel_id=1, source_target_pairs={{0,1},{1,2},{2,3},{3,4},{4,5},{5,6},{6,7},{7,0},{8,9},{9,10},{10,1... | collective-permute-start | bytes 3145736 | tf_op jit(solution)/shard_map/ppermute | solution.py:67
  7.2 25.5 %collective-permute-start.1 = (bf16[128,4096]{1,0:T(8,128)(2,1)}, bf16[128,4096]{1,0:T(8,128)(2,1)S(1)}, u32[]{:S(2)}, u32[]{:S(2)}) collective-permute-start(bf16[128,4096]{1,0:T(8,128)(2,1)} %param.3), channel_id=1, source_target_pairs={{0,7},{1,0},{2,1},{3,2},{4,3},{5,4},{6,5},{7,6},{8,15},{9,8},{10,9... | collective-permute-start | bytes 3145736 | tf_op jit(solution)/shard_map/ppermute | solution.py:74
  10.8 24.8 %copy-start = (bf16[1024,1792]{1,0:T(8,128)(2,1)S(1)}, bf16[1024,1792]{1,0:T(8,128)(2,1)}, u32[]{:S(2)}) copy-start(bf16[1024,1792]{1,0:T(8,128)(2,1)} %param.4) | copy-start | bytes 11010052
  23.6 15.8 %collective-permute-start.2 = (bf16[128,4096]{1,0:T(8,128)(2,1)}, bf16[128,4096]{1,0:T(8,128)(2,1)}, u32[]{:S(2)}, u32[]{:S(2)}) collective-permute-start(bf16[128,4096]{1,0:T(8,128)(2,1)} %collective-permute-done), channel_id=1, source_target_pairs={{0,1},{1,2},{2,3},{3,4},{4,5},{5,6},{6,7},{7,0},{8,9},{9,10},{10,1... | collective-permute-start | bytes 3145736 | tf_op jit(solution)/shard_map/ppermute | solution.py:67
  32.7 15.3 %collective-permute-start.3 = (bf16[128,4096]{1,0:T(8,128)(2,1)S(1)}, bf16[128,4096]{1,0:T(8,128)(2,1)S(1)}, u32[]{:S(2)}, u32[]{:S(2)}) collective-permute-start(bf16[128,4096]{1,0:T(8,128)(2,1)S(1)} %collective-permute-done.1), channel_id=1, source_target_pairs={{0,7},{1,0},{2,1},{3,2},{4,3},{5,4},{6,5},{7,6},{8,15},{9,8},{10,9... | collective-permute-start | bytes 3145736 | tf_op jit(solution)/shard_map/ppermute | solution.py:74
  39.4 15.6 %collective-permute-start.4 = (bf16[128,4096]{1,0:T(8,128)(2,1)}, bf16[128,4096]{1,0:T(8,128)(2,1)S(1)}, u32[]{:S(2)}, u32[]{:S(2)}) collective-permute-start(bf16[128,4096]{1,0:T(8,128)(2,1)} %collective-permute-done.2), channel_id=1, source_target_pairs={{0,1},{1,2},{2,3},{3,4},{4,5},{5,6},{6,7},{7,0},{8,9},{9,10},{10,1... | collective-permute-start | bytes 3145736 | tf_op jit(solution)/shard_map/ppermute | solution.py:67
  48.0 15.4 %collective-permute-start.5 = (bf16[128,4096]{1,0:T(8,128)(2,1)S(1)}, bf16[128,4096]{1,0:T(8,128)(2,1)S(1)}, u32[]{:S(2)}, u32[]{:S(2)}) collective-permute-start(bf16[128,4096]{1,0:T(8,128)(2,1)S(1)} %collective-permute-done.3), channel_id=1, source_target_pairs={{0,7},{1,0},{2,1},{3,2},{4,3},{5,4},{6,5},{7,6},{8,15},{9,8},{10,9... | collective-permute-start | bytes 3145736 | tf_op jit(solution)/shard_map/ppermute | solution.py:74
  55.0 15.4 %collective-permute-start.6 = (bf16[128,4096]{1,0:T(8,128)(2,1)S(1)}, bf16[128,4096]{1,0:T(8,128)(2,1)S(1)}, u32[]{:S(2)}, u32[]{:S(2)}) collective-permute-start(bf16[128,4096]{1,0:T(8,128)(2,1)S(1)} %collective-permute-done.4), channel_id=1, source_target_pairs={{0,1},{1,2},{2,3},{3,4},{4,5},{5,6},{6,7},{7,0},{8,9},{9,10},{10,1... | collective-permute-start | bytes 3145736 | tf_op jit(solution)/shard_map/ppermute | solution.py:67
  159.1 26.6 %all-to-all-start.3 = ((bf16[8,512,64]{1,2,0:T(8,128)(2,1)}), bf16[8,512,64]{1,2,0:T(8,128)(2,1)S(1)}, u32[]{:S(2)}, u32[]{:S(2)}) async-start(bf16[8,512,64]{1,2,0:T(8,128)(2,1)} %broadcast_in_dim.13), calls=%async_computation.3 | async-start | bytes 1048576 | tf_op jit(solution)/shard_map/all_to_all | solution.py:20
  162.6 118.7 %all-reduce.2.cloned.1.call-start = ((), (), s32[]{:S(2)}) async-start(), calls=%async_computation.4 | async-start | bytes 917504 | tf_op jit(solution)/shard_map/psum | solution.py:100
  282.3 17.3 %copy-start.2 = (f32[1792,64]{0,1:T(8,128)}, f32[1792,64]{0,1:T(8,128)S(1)}, u32[]{:S(2)}) copy-start(f32[1792,64]{0,1:T(8,128)S(1)} %broadcast_multiply_fusion) | copy-start | bytes 1376260
Sparse Core Ops, SparseCore 0:
  198.7 82.5 all-reduce.1
